TPU v7x, 32 devices: a whole 2x2x4 slice. The times are simulated.
32 devices in a mesh: pairs: 8 (over y, x, core), aux: 4 (over z).
Axes of the slice: x: 2, y: 2, z: 4, core: 2. Of those that a mesh axis runs over, the one named last changes fastest.
Arguments:
- factors: bfloat16 [4096, 128, 128], P('aux', 'pairs'), may hold values from -1 to 1
- coefficients: bfloat16 [128, 256, 128], P(('pairs', 'aux')), may hold values from -0.375 to 0.375
- amplitudes: bfloat16 [128, 128, 128], P(('pairs', 'aux')), may hold values from -6 to 6
- domains: int32 [128, 256], P(('pairs', 'aux')), may hold values from 0 to 573, as said below
- partners: int32 [128, 12], P(('pairs', 'aux')), may hold values from 0 to 127, as said below
- couplings: float32 [128, 12], P(('pairs', 'aux')), may hold values from -4 to 4
- energies: float32 [128, 128], P(('pairs', 'aux')), may hold values from 0.5 to 4
Outputs:
- residual: float32 [128, 128, 128], P(('pairs', 'aux'))
Inputs may be any that keep to these rules, and one draw needn't show every extreme that they name: `partners`: row p names 12 different pairs other than p, all within the run of 17 consecutive pair numbers centred on p, moved inward where it would pass 0 or 127. `domains`: each row holds 256 different function numbers.
All inputs are finite; a program needn't handle non-finite values.
Results may differ from a plain program's by a relative error of at most 0.0065.
Values may be sent and summed in bfloat16 or wider, within the bound.
No kernel may reach another device: no remote copies, remote signals or barrier semaphores. Data moves between devices by JAX's collectives and lax.ppermute only.
A program may use at most 128 MiB of HBM per device.

v0:
```python
import jax
import jax.numpy as jnp
from jax import lax
from jax.sharding import PartitionSpec as P


def shortened(shard):
    return jax.tree.map(lambda a: a.astype(jnp.bfloat16) if a.dtype == jnp.float32 else a, shard)


def extended(cells, sides, width):
    for axis, dim in sides:
        count = lax.axis_size(axis)
        ends = count - 1
        head = lax.slice_in_dim(cells, 0, width, axis=dim)
        tail = lax.slice_in_dim(cells, cells.shape[dim] - width, cells.shape[dim], axis=dim)
        cells = jnp.concatenate(
            [
                lax.ppermute(tail, axis, [(i, (i + 1) % count) for i in range(ends)]),
                cells,
                lax.ppermute(head, axis, [((i + 1) % count, i) for i in range(ends)]),
            ],
            axis=dim,
        )
    return cells


def shards(factors, coefficients, amplitudes, domains, partners, couplings, energies):
    own_pairs = amplitudes.shape[0]
    dom_width = coefficients.shape[1]
    aux_count = lax.axis_size("aux")
    group_size = own_pairs * aux_count
    reach_pairs = group_size // 2
    group_index = lax.axis_index("pairs")
    partial_value = jnp.einsum("xpa,xpb->pab", factors, factors, preferred_element_type=jnp.float32)
    partial_value = lax.optimization_barrier(partial_value.astype(jnp.bfloat16)).astype(jnp.float32)
    exchange_k = lax.psum_scatter(
        partial_value.astype(jnp.bfloat16), "aux", scatter_dimension=0, tiled=True
    ).astype(jnp.float32)
    stacked = jnp.concatenate([coefficients, amplitudes], axis=1)
    gathered = (
        lax.all_gather(stacked, "aux", axis=0, tiled=True),
        lax.all_gather(domains, "aux", axis=0, tiled=True),
    )
    window_rows, window_funcs = [
        extended(shortened(member), (("pairs", 0),), reach_pairs).astype(member.dtype)
        for member in gathered
    ]
    first_pair = group_index * group_size - reach_pairs
    slots = partners - first_pair
    far_rows = window_rows[slots]
    far_funcs = window_funcs[slots]
    far_coeff = far_rows[:, :, :dom_width]
    far_amps = far_rows[:, :, dom_width:]
    matches = (domains[:, None, :, None] == far_funcs[:, :, None, :]).astype(jnp.bfloat16)
    matched = jnp.einsum(
        "pcfg,pcgn->pcfn", matches, far_coeff, preferred_element_type=jnp.float32
    ).astype(jnp.bfloat16)
    intersection = jnp.einsum(
        "pfa,pcfn->pcan", coefficients, matched, preferred_element_type=jnp.float32
    ).astype(jnp.bfloat16)
    mixed_rows = jnp.einsum(
        "pcan,pcnm->pcam", intersection, far_amps, preferred_element_type=jnp.float32
    ).astype(jnp.bfloat16)
    coupled = jnp.einsum(
        "pcam,pcbm->pcab", mixed_rows, intersection, preferred_element_type=jnp.float32
    )
    cycle_term = jnp.sum(couplings[:, :, None, None] * coupled, axis=1)
    diagonal_term = (energies[:, :, None] + energies[:, None, :]) * amplitudes.astype(jnp.float32)
    return exchange_k + diagonal_term - cycle_term


def solution(mesh):
    return jax.shard_map(
        shards,
        mesh=mesh,
        in_specs=(
            P("aux", "pairs", None),
            P(("pairs", "aux"), None, None),
            P(("pairs", "aux"), None, None),
            P(("pairs", "aux"), None),
            P(("pairs", "aux"), None),
            P(("pairs", "aux"), None),
            P(("pairs", "aux"), None),
        ),
        out_specs=P(("pairs", "aux"), None, None),
        check_vma=False,
    )
```

profile of v0, /device:TPU:0, one launch (start us, length us, event | category | flops | bytes accessed | tf_op | source)
XLA Modules:
  0.0 94.0 jit_solution(6787805975083660309)
XLA Ops:
  6.5 0.0 all-gather.3.cloned.1.call-start
  6.5 1.8 %pad_maximum_fusion.1 = bf16[4,384,128]{2,1,0:T(8,128)(2,1)} fusion(bf16[4,128,128]{2,1,0:T(8,128)(2,1)} %param.9, bf16[4,256,128]{2,1,0:T(8,128)(2,1)} %param.8), kind=kLoop, calls=%fused_computation.17 | loop fusion | flops 786432 | bytes 786432 | tf_op jit(solution)/shard_map/concatenate | solution.py:40
  8.3 0.0 all-gather.3.cloned.1.call-update
  8.3 0.0 reduce-scatter.2.cloned.1.call-start
  8.4 15.1 %all-gather = s32[4,4,256]{2,1,0:T(4,128)S(1)} all-gather(s32[1,4,256]{2,1,0:T(4,128)} %bitcast.11), channel_id=1, replica_groups=mesh['pairs'=8,'aux'=4] {'aux'}, dimensions={0}, use_global_device_ids=true | all-gather | bytes 20480 | tf_op jit(solution)/shard_map/all_gather | solution.py:43
  23.6 1.3 %collective-permute-start = (s32[8,256]{1,0:T(8,128)S(1)}, s32[8,256]{1,0:T(8,128)S(1)}, u32[]{:S(2)}, u32[]{:S(2)}) collective-permute-start(s32[8,256]{1,0:T(8,128)S(1)} %reshape.27), channel_id=1, source_target_pairs={{0,4},{4,8},{8,12},{12,16},{16,20},{20,24},{24,28},{1,5},{5,9},{9,... | collective-permute-start | bytes 24584 | tf_op jit(solution)/shard_map/ppermute | solution.py:19
  24.9 1.3 %collective-permute-start.1 = (s32[8,256]{1,0:T(8,128)S(1)}, s32[8,256]{1,0:T(8,128)S(1)}, u32[]{:S(2)}, u32[]{:S(2)}) collective-permute-start(s32[8,256]{1,0:T(8,128)S(1)} %reshape.28), channel_id=1, source_target_pairs={{4,0},{8,4},{12,8},{16,12},{20,16},{24,20},{28,24},{5,1},{9,5},{13... | collective-permute-start | bytes 24584 | tf_op jit(solution)/shard_map/ppermute | solution.py:21
  26.2 22.6 %all-gather.3.cloned.1.call-done = bf16[16,384,128]{2,1,0:T(8,128)(2,1)} async-done(((bf16[4,384,128]{2,1,0:T(8,128)(2,1)}), bf16[16,384,128]{2,1,0:T(8,128)(2,1)}) %all-gather.3.cloned.1.call-update) | async-done | bytes 1572880 | tf_op jit(solution)/shard_map/all_gather | solution.py:42
  48.7 1.5 %fusion.31 = (bf16[8,384,128]{2,1,0:T(8,128)(2,1)S(1)}, bf16[8,384,128]{2,1,0:T(8,128)(2,1)S(1)}) fusion(bf16[16,384,128]{2,1,0:T(8,128)(2,1)} %all-gather.3.cloned.1.call-done), kind=kLoop, calls=%fused_computation.23 | loop fusion | bytes 3145728 | tf_op jit(solution)/shard_map/slice | solution.py:16
  50.2 1.4 %collective-permute-start.2 = (bf16[8,384,128]{2,1,0:T(8,128)(2,1)S(1)}, bf16[8,384,128]{2,1,0:T(8,128)(2,1)S(1)}, u32[]{:S(2)}, u32[]{:S(2)}) collective-permute-start(bf16[8,384,128]{2,1,0:T(8,128)(2,1)S(1)} %get-tuple-element.5), channel_id=1, source_target_pairs={{0,4},{4,8},{8,12},{12,16},{16,20},{20,24},{24,28},{1,5},{5,9},{9,... | collective-permute-start | bytes 2359304 | tf_op jit(solution)/shard_map/ppermute | solution.py:19
  51.7 0.0 copy-start.5
  51.7 1.3 %collective-permute-start.3 = (bf16[8,384,128]{2,1,0:T(8,128)(2,1)S(1)}, bf16[8,384,128]{2,1,0:T(8,128)(2,1)}, u32[]{:S(2)}, u32[]{:S(2)}) collective-permute-start(bf16[8,384,128]{2,1,0:T(8,128)(2,1)S(1)} %get-tuple-element.6), channel_id=1, source_target_pairs={{4,0},{8,4},{12,8},{16,12},{20,16},{24,20},{28,24},{5,1},{9,5},{13... | collective-permute-start | bytes 2359304 | tf_op jit(solution)/shard_map/ppermute | solution.py:21
  53.0 8.7 %fusion.25 = bf16[16,128,128]{2,1,0:T(8,128)(2,1)} fusion(bf16[1024,16,128]{2,1,0:T(8,128)(2,1)} %param.7), kind=kOutput, calls=%fused_computation.16 | convolution fusion | flops 537133056 | bytes 4718592 | tf_op jit(solution)/shard_map/xpa,xpb->pab/dot_general | solution.py:35
  61.6 0.0 reduce-scatter.2.cloned.1.call-update
  61.7 0.0 copy-done.5
  61.7 0.1 reshape.7
  61.8 0.0 collective-permute-done
  61.8 0.0 collective-permute-done.1
  61.8 0.6 gather_fusion
  62.5 0.0 collective-permute-done.2
  62.5 0.0 copy-start
  62.5 0.9 copy-done
  63.4 0.0 collective-permute-done.3
  63.4 2.0 %pad_maximum_fusion = bf16[32,384,128]{2,1,0:T(8,128)(2,1)S(1)} fusion(bf16[8,384,128]{2,1,0:T(8,128)(2,1)} %collective-permute-done.3, bf16[16,384,128]{2,1,0:T(8,128)(2,1)} %all-gather.3.cloned.1.call-done, bf16[8,384,128]{2,1,0:T(8,128)(2,1)} %copy-done), kind=kLoop, calls=%fused_computation.9 | loop fusion | flops 3145728 | bytes 6291456 | tf_op jit(solution)/shard_map/concatenate | solution.py:17
  65.4 0.0 copy-start.2
  65.4 0.0 copy-start.4
  65.4 3.4 %gather_fusion.1 = bf16[48,384,128]{2,1,0:T(8,128)(2,1)} fusion(bf16[32,384,128]{2,1,0:T(8,128)(2,1)S(1)} %pad_maximum_fusion, s32[1024]{0:T(1024)S(1)} %pad_clamp_fusion), kind=kCustom, calls=%fused_computation.1 | custom fusion | bytes 9437376 | tf_op jit(solution)/shard_map/gather | solution.py:51
  68.9 0.0 copy-done.2
  68.9 0.0 copy-done.4
  68.9 0.0 copy-start.6
  68.9 4.9 %fusion.17 = bf16[4,12,128,128]{3,2,1,0:T(8,128)(2,1)S(1)} fusion(bf16[4,12,384,128]{3,2,1,0:T(8,128)(2,1)} %bitcast.9, s32[4,12,256]{2,1,0:T(8,128)S(1)} %reshape.6, s32[4,256]{1,0:T(4,128)S(1)} %copy-done.4, bf16[4,256,128]{2,1,0:T(8,128)(2,1)S(1)} %copy-done.2), kind=kOutput, calls=%fused_computation.13 | convolution fusion | flops 1213464576 | bytes 5033984 | tf_op jit(solution)/shard_map/pfa,pcfn->pcan/dot_general | solution.py:59
  73.8 0.0 copy-done.6
  73.8 0.0 copy-start.1
  73.8 0.0 copy-start.3
  73.8 2.6 %multiply_reduce_fusion = f32[4,128,128]{2,1,0:T(8,128)S(1)} fusion(bf16[4,12,128,128]{3,2,1,0:T(8,128)(2,1)S(1)} %fusion.17, f32[4,12]{1,0:T(4,128)S(1)} %copy-done.6, bf16[4,12,384,128]{3,2,1,0:T(8,128)(2,1)} %bitcast.10), kind=kOutput, calls=%fused_computation.10 | convolution fusion | flops 404946944 | bytes 4982784 | tf_op jit(solution)/shard_map/pcam,pcbm->pcab/dot_general | solution.py:65
  76.5 9.0 %reduce-scatter.2.cloned.1.call-done = bf16[4,128,128]{2,1,0:T(8,128)(2,1)} async-done(((bf16[16,128,128]{2,1,0:T(8,128)(2,1)}), bf16[4,128,128]{2,1,0:T(8,128)(2,1)}) %reduce-scatter.2.cloned.1.call-update) | async-done | bytes 131088 | tf_op jit(solution)/shard_map/reduce_scatter | solution.py:37
  85.5 0.0 copy-done.1
  85.5 0.0 copy-done.3
  85.5 1.7 %add_subtract_fusion = f32[4,128,128]{2,1,0:T(8,128)} fusion(f32[4,128,128]{2,1,0:T(8,128)S(1)} %multiply_reduce_fusion, bf16[4,128,128]{2,1,0:T(8,128)(2,1)S(1)} %copy-done.1, bf16[4,128,128]{2,1,0:T(8,128)(2,1)} %reduce-scatter.2.cloned.1.call-done, f32[4,128]{1,0:T(4,128)S(1)} %copy-done.3), kind=kLoop, calls=%fused_computation.19 | loop fusion | flops 393216 | bytes 788480 | tf_op jit(solution)/shard_map/sub | solution.py:70
  (8 shorter events, 0.1 us)
Async XLA Ops:
  6.5 42.2 %all-gather.3.cloned.1.call-start = ((), (), s32[]{:S(2)}) async-start(), calls=%async_computation.2 | async-start | bytes 1966080 | tf_op jit(solution)/shard_map/all_gather | solution.py:42
  8.3 77.1 %reduce-scatter.2.cloned.1.call-start = ((), (), s32[]{:S(2)}) async-start(), calls=%async_computation.1 | async-start | bytes 655360 | tf_op jit(solution)/shard_map/reduce_scatter | solution.py:37
  23.6 38.2 %collective-permute-start = (s32[8,256]{1,0:T(8,128)S(1)}, s32[8,256]{1,0:T(8,128)S(1)}, u32[]{:S(2)}, u32[]{:S(2)}) collective-permute-start(s32[8,256]{1,0:T(8,128)S(1)} %reshape.27), channel_id=1, source_target_pairs={{0,4},{4,8},{8,12},{12,16},{16,20},{20,24},{24,28},{1,5},{5,9},{9,... | collective-permute-start | bytes 24584 | tf_op jit(solution)/shard_map/ppermute | solution.py:19
  24.9 36.9 %collective-permute-start.1 = (s32[8,256]{1,0:T(8,128)S(1)}, s32[8,256]{1,0:T(8,128)S(1)}, u32[]{:S(2)}, u32[]{:S(2)}) collective-permute-start(s32[8,256]{1,0:T(8,128)S(1)} %reshape.28), channel_id=1, source_target_pairs={{4,0},{8,4},{12,8},{16,12},{20,16},{24,20},{28,24},{5,1},{9,5},{13... | collective-permute-start | bytes 24584 | tf_op jit(solution)/shard_map/ppermute | solution.py:21
  50.2 12.2 %collective-permute-start.2 = (bf16[8,384,128]{2,1,0:T(8,128)(2,1)S(1)}, bf16[8,384,128]{2,1,0:T(8,128)(2,1)S(1)}, u32[]{:S(2)}, u32[]{:S(2)}) collective-permute-start(bf16[8,384,128]{2,1,0:T(8,128)(2,1)S(1)} %get-tuple-element.5), channel_id=1, source_target_pairs={{0,4},{4,8},{8,12},{12,16},{16,20},{20,24},{24,28},{1,5},{5,9},{9,... | collective-permute-start | bytes 2359304 | tf_op jit(solution)/shard_map/ppermute | solution.py:19
  51.7 10.0 %copy-start.5 = (s32[4,12]{1,0:T(4,128)S(1)}, s32[4,12]{1,0:T(4,128)}, u32[]{:S(2)}) copy-start(s32[4,12]{1,0:T(4,128)} %param.11) | copy-start | bytes 580
  51.7 11.7 %collective-permute-start.3 = (bf16[8,384,128]{2,1,0:T(8,128)(2,1)S(1)}, bf16[8,384,128]{2,1,0:T(8,128)(2,1)}, u32[]{:S(2)}, u32[]{:S(2)}) collective-permute-start(bf16[8,384,128]{2,1,0:T(8,128)(2,1)S(1)} %get-tuple-element.6), channel_id=1, source_target_pairs={{4,0},{8,4},{12,8},{16,12},{20,16},{24,20},{28,24},{5,1},{9,5},{13... | collective-permute-start | bytes 2359304 | tf_op jit(solution)/shard_map/ppermute | solution.py:21
  62.5 0.9 copy-start
  65.4 3.5 %copy-start.2 = (bf16[4,256,128]{2,1,0:T(8,128)(2,1)S(1)}, bf16[4,256,128]{2,1,0:T(8,128)(2,1)}, u32[]{:S(2)}) copy-start(bf16[4,256,128]{2,1,0:T(8,128)(2,1)} %param.8) | copy-start | bytes 786436
  65.4 3.5 %copy-start.4 = (s32[4,256]{1,0:T(4,128)S(1)}, s32[4,256]{1,0:T(4,128)}, u32[]{:S(2)}) copy-start(s32[4,256]{1,0:T(4,128)} %param.10) | copy-start | bytes 12292
  68.9 4.9 %copy-start.6 = (f32[4,12]{1,0:T(4,128)S(1)}, f32[4,12]{1,0:T(4,128)}, u32[]{:S(2)}) copy-start(f32[4,12]{1,0:T(4,128)} %param.12) | copy-start | bytes 580
  73.8 11.7 %copy-start.1 = (bf16[4,128,128]{2,1,0:T(8,128)(2,1)S(1)}, bf16[4,128,128]{2,1,0:T(8,128)(2,1)}, u32[]{:S(2)}) copy-start(bf16[4,128,128]{2,1,0:T(8,128)(2,1)} %param.9) | copy-start | bytes 393220
  73.8 11.6 %copy-start.3 = (f32[4,128]{1,0:T(4,128)S(1)}, f32[4,128]{1,0:T(4,128)}, u32[]{:S(2)}) copy-start(f32[4,128]{1,0:T(4,128)} %param.13) | copy-start | bytes 6148
Sparse Core Ops, SparseCore 0:
  8.9 39.7 all-gather.2
  61.8 23.6 reduce-scatter.1
where the time goes:
time: 94.6 us; the launch traced here: 94 us
  waiting for transfers between devices  31.6 us (33%)
  matrix products  16.2 us (17%)
  blocking collectives  15.1 us (16%)
  between operations  13.6 us (14%)
  local copies, waits for them, and re-layouts  6.61 us (7%)
  other arithmetic  5.58 us (6%)
  starting transfers between devices  5.32 us (6%)
    all_gather x1, waiting for transfers between devices, shards(): lax.all_gather(stacked, 'aux', axis=0, tiled=True)  22.6 us
    all_gather x1, blocking collectives, shards(): lax.all_gather(domains, 'aux', axis=0, tiled=True)  15.1 us
    reduce_scatter x1, waiting for transfers between devices, shards(): lax.psum_scatter(partial_value.astype(jnp.bfloat16), 'aux', scatter_dimen...  9.01 us
    dot_general x1, matrix products, shards(): jnp.einsum('xpa,xpb->pab', factors, factors, preferred_element_type=jnp.f...  8.66 us
    dot_general x1, matrix products, shards(): jnp.einsum('pfa,pcfn->pcan', coefficients, matched, preferred_element_typ...  4.9 us
    gather x1, local copies, waits for them, and re-layouts, shards(): far_rows = window_rows[slots]  3.43 us
    ppermute x2, starting transfers between devices, extended(): lax.ppermute(tail, axis, [(i, (i + 1) % count) for i in range(ends)])  2.69 us
    dot_general x1, matrix products, shards(): jnp.einsum('pcam,pcbm->pcab', mixed_rows, intersection, preferred_element...  2.62 us
  transfers between devices with their start and end apart: 6, of which 2 were waited for; matrix products, arithmetic and copies ran while one was open for 25% of the time, Pallas kernels for 0%

commit v1 on v0

v1 whole, which is shorter than its diff:
```python
import functools

import jax
import jax.numpy as jnp
from jax import lax
from jax.experimental import pallas as pl
from jax.experimental.pallas import tpu as pltpu
from jax.sharding import PartitionSpec as P

BF16 = jnp.bfloat16
F32 = jnp.float32
WHOLE = pl.BlockSpec(memory_space=pltpu.VMEM)


def meta_rows(dom_width, lanes, weight_count):
    rows = 2 * (dom_width // lanes) + 2 * -(-weight_count // lanes)
    return -(-rows // 16) * 16


def pack_body(ids, coeff, amps, dom, partners, couplings, sent, hosted, *, aux_count):
    own, width, lanes = coeff.shape
    slots = 2 * own
    group = own * aux_count
    weight_rows = -(-aux_count * slots // lanes)
    at = lax.broadcasted_iota(jnp.int32, (1, weight_rows * lanes), 1)
    host, slot = at // slots, at % slots
    first = ids[0] + host * own
    beside = jnp.where(host < aux_count // 2, group, -group)
    number = jnp.where(slot < own, first + slot, first + slot - own + beside)
    number = jnp.where(host < aux_count, number, -1)
    listed, strength = partners[...], couplings[...]
    weight = jnp.zeros((own, weight_rows * lanes), F32)
    for c in range(listed.shape[1]):
        weight += jnp.where(listed[:, c : c + 1] == number, strength[:, c : c + 1], 0.0)
    coarse = weight.astype(BF16).astype(F32)
    fine = weight - coarse
    funcs = dom[...]
    high = (funcs >> 8).astype(F32)
    low = (funcs & 255).astype(F32)
    extra = meta_rows(width, lanes, aux_count * slots)
    for p in range(own):
        rows = []
        for part in (high, low, coarse, fine):
            for k in range(part.shape[1] // lanes):
                rows.append(part[p : p + 1, k * lanes : (k + 1) * lanes])
        rows.append(jnp.zeros((extra - len(rows), lanes), F32))
        meta = jnp.concatenate(rows, axis=0).astype(BF16)
        orbitals = coeff[p]
        sent[p, :width] = orbitals
        sent[p, width:] = meta
        hosted[p, :width] = orbitals
        hosted[p, width : width + extra] = meta
        hosted[p, width + extra :] = amps[p]


def functions_of(meta, width, lanes):
    parts = width // lanes
    return [meta[k : k + 1] * 256.0 + meta[parts + k : parts + k + 1] for k in range(parts)]


def terms_body(ids, sent, near, beside, exchange, out, *, width):
    own, _, lanes = sent.shape
    extra = sent.shape[1] - width
    slots = 2 * own
    parts = width // lanes
    place = ids[0] * slots
    sources = [(near, j) for j in range(own)] + [(beside, j) for j in range(own)]
    far_funcs = []
    for ref, j in sources:
        meta = ref[j, width : width + extra].astype(F32)
        far_funcs.append(jnp.concatenate(functions_of(meta, width, lanes), axis=1))
    for p in range(own):
        meta = sent[p, width:].astype(F32)
        funcs = jnp.concatenate(functions_of(meta, width, lanes), axis=1)
        column = jnp.transpose(jnp.broadcast_to(funcs, (8, width)))[:, :1]
        weights = meta[2 * parts : 2 * parts + 1] + meta[2 * parts + 1 : 2 * parts + 2]
        lane = lax.broadcasted_iota(jnp.int32, (1, lanes), 1)
        matched = []
        for (ref, j), row in zip(sources, far_funcs):
            same = jnp.where(column == row, 1.0, 0.0).astype(BF16)
            matched.append(
                jnp.dot(same, ref[j, :width], preferred_element_type=F32).astype(BF16)
            )
        overlap = lax.dot_general(
            sent[p, :width],
            jnp.concatenate(matched, axis=1),
            (((0,), (0,)), ((), ())),
            preferred_element_type=F32,
        ).astype(BF16)
        mixed = []
        for k, (ref, j) in enumerate(sources):
            weight = jnp.sum(jnp.where(lane == place + k, weights, 0.0), axis=1, keepdims=True)
            part = jnp.dot(
                overlap[:, k * lanes : (k + 1) * lanes],
                ref[j, width + extra :],
                preferred_element_type=F32,
            )
            mixed.append((part * weight).astype(BF16))
        coupled = lax.dot_general(
            jnp.concatenate(mixed, axis=1),
            overlap,
            (((1,), (1,)), ((), ())),
            preferred_element_type=F32,
        )
        out[p] = (exchange[p] - coupled).astype(out.dtype)


def shards(factors, coefficients, amplitudes, domains, partners, couplings, energies):
    own, width, lanes = coefficients.shape
    aux_count = lax.axis_size("aux")
    group_count = lax.axis_size("pairs")
    half = aux_count // 2
    extra = meta_rows(width, lanes, aux_count * 2 * own)
    group_at = lax.axis_index("pairs")
    aux_at = lax.axis_index("aux")
    smem = pl.BlockSpec(memory_space=pltpu.SMEM)

    sent, hosted = pl.pallas_call(
        functools.partial(pack_body, aux_count=aux_count),
        out_shape=(
            jax.ShapeDtypeStruct((own, width + extra, lanes), BF16),
            jax.ShapeDtypeStruct((own, width + extra + lanes, lanes), BF16),
        ),
        in_specs=[smem, WHOLE, WHOLE, WHOLE, WHOLE, WHOLE],
        out_specs=(WHOLE, WHOLE),
        name="pack",
    )(
        (group_at * own * aux_count).reshape(1).astype(jnp.int32),
        coefficients, amplitudes, domains, partners, couplings,
    )

    routes = []
    for g in range(group_count):
        for z in range(aux_count):
            to = g - 1 if z < half else g + 1
            if 0 <= to < group_count:
                routes.append((g * aux_count + z, to * aux_count + z))
    beside = lax.ppermute(hosted, ("pairs", "aux"), routes)
    order = sorted(range(1, aux_count), key=lambda s: -min(s, aux_count - s))
    arrived = {0: sent}
    for s in order:
        arrived[s] = lax.ppermute(sent, "aux", [((i + s) % aux_count, i) for i in range(aux_count)])

    exchange = jnp.einsum("xpa,xpb->pab", factors, factors, preferred_element_type=F32)

    def terms(s, dtype):
        ids = jnp.stack([aux_at, (aux_at + s) % aux_count]).astype(jnp.int32)
        whole = lambda a: pl.BlockSpec(a.shape, lambda i, ids: (0,) * a.ndim)
        return pl.pallas_call(
            functools.partial(terms_body, width=width),
            grid_spec=pltpu.PrefetchScalarGridSpec(
                num_scalar_prefetch=1,
                grid=(1,),
                in_specs=[
                    whole(arrived[s]), whole(hosted), whole(beside),
                    pl.BlockSpec((own, lanes, lanes), lambda i, ids: (ids[1], 0, 0)),
                ],
                out_specs=pl.BlockSpec((own, lanes, lanes), lambda i, ids: (0, 0, 0)),
            ),
            out_shape=jax.ShapeDtypeStruct((own, lanes, lanes), dtype),
            name="terms",
        )(ids, arrived[s], hosted, beside, exchange)

    returned = [
        lax.ppermute(terms(s, BF16), "aux", [(i, (i + s) % aux_count) for i in range(aux_count)])
        for s in order
    ]
    total = terms(0, F32)
    total += (energies[:, :, None] + energies[:, None, :]) * amplitudes.astype(F32)
    for part in returned:
        total += part.astype(F32)
    return total


def solution(mesh):
    return jax.shard_map(
        shards,
        mesh=mesh,
        in_specs=(
            P("aux", "pairs", None),
            P(("pairs", "aux"), None, None),
            P(("pairs", "aux"), None, None),
            P(("pairs", "aux"), None),
            P(("pairs", "aux"), None),
            P(("pairs", "aux"), None),
            P(("pairs", "aux"), None),
        ),
        out_specs=P(("pairs", "aux"), None, None),
        check_vma=False,
    )
```

time: 94.6 us -> 58.3 us (0.62)
  waiting for transfers between devices: 31.6 us -> 0.02 us
  Pallas kernels: 0 us -> 24.8 us
  blocking collectives: 15.1 us -> 0 us
  between operations: 13.6 us -> 0.09 us
  starting transfers between devices: 5.32 us -> 17.3 us
  matrix products: 16.2 us -> 8.62 us
  local copies, waits for them, and re-layouts: 6.61 us -> 2.9 us
  other arithmetic: 5.58 us -> 4.25 us
    pallas_call x0 -> x5, Pallas kernels: none -> 24.8 us  [the longest x4 22.8 us: terms(): pl.pallas_call(functools.partial(terms_body, width=width), grid_spec=pltp...]
    all_gather x1 -> x0, waiting for transfers between devices: 22.6 us -> none  [shards(): lax.all_gather(stacked, 'aux', axis=0, tiled=True)]
    all_gather x1 -> x0, blocking collectives: 15.1 us -> none  [shards(): lax.all_gather(domains, 'aux', axis=0, tiled=True)]
    ppermute x4 -> x7, starting transfers between devices: 5.28 us -> 17.3 us  [the longest x3 9.89 us: shards(): lax.ppermute(terms(s, BF16), 'aux', [(i, (i + s) % aux_count) for i in ra...]
    reduce_scatter x1 -> x0, waiting for transfers between devices: 9.01 us -> none  [shards(): lax.psum_scatter(partial_value.astype(jnp.bfloat16), 'aux', scatter_dimen...]
    dot_general x3 -> x1, matrix products: 16.2 us -> 8.62 us  [shards(): jnp.einsum('xpa,xpb->pab', factors, factors, preferred_element_type=F32)]
    gather x3 -> x0, local copies, waits for them, and re-layouts: 4.07 us -> none  [the longest x1 3.43 us: shards(): far_rows = window_rows[slots]]
    concatenate x3 -> x0, other arithmetic: 3.82 us -> none  [the longest x2 2.04 us: extended(): jnp.concatenate([lax.ppermute(tail, axis, [(i, (i + 1) % count) for i in...]
  transfers between devices with their start and end apart: 6 -> 7, of which waited for: 2 -> 0; matrix products, arithmetic and copies ran while one was open for 25% -> 19% of each run, Pallas kernels for 0% -> 39%
where the time goes in v1:
time: 58.3 us; the launch traced here: 57.9 us
  Pallas kernels  24.8 us (43%)
  starting transfers between devices  17.3 us (30%)
  matrix products  8.62 us (15%)
  other arithmetic  4.25 us (7%)
  local copies, waits for them, and re-layouts  2.9 us (5%)
    pallas_call x4, Pallas kernels, terms(): pl.pallas_call(functools.partial(terms_body, width=width), grid_spec=pltp...  22.8 us
    ppermute x3, starting transfers between devices, shards(): lax.ppermute(terms(s, BF16), 'aux', [(i, (i + s) % aux_count) for i in ra...  9.89 us
    dot_general x1, matrix products, shards(): jnp.einsum('xpa,xpb->pab', factors, factors, preferred_element_type=F32)  8.62 us
    ppermute x3, starting transfers between devices, shards(): lax.ppermute(sent, 'aux', [((i + s) % aux_count, i) for i in range(aux_co...  6.09 us
    unnamed x12, local copies, waits for them, and re-layouts  2.9 us
    another operation x4, other arithmetic, terms(): ids = jnp.stack([aux_at, (aux_at + s) % aux_count]).astype(jnp.int32)  2.42 us
    pallas_call x1, Pallas kernels, shards(): pl.pallas_call(functools.partial(pack_body, aux_count=aux_count), out_sha...  2.03 us
    add x1, other arithmetic, shards(): total += part.astype(F32)  1.83 us
  transfers between devices with their start and end apart: 7, of which 0 were waited for; matrix products, arithmetic and copies ran while one was open for 19% of the time, Pallas kernels for 39%

profile of v1, /device:TPU:0, one launch (start us, length us, event | category | flops | bytes accessed | tf_op | source)
XLA Modules:
  0.0 57.9 jit_solution(163375210523692160)
XLA Ops:
  0.0 2.0 %pack.1 = (bf16[4,272,128]{2,1,0:T(8,128)(2,1)}, bf16[4,400,128]{2,1,0:T(8,128)(2,1)}) custom-call(s32[1]{0:T(128)} %bitcast.2.ids, bf16[4,256,128]{2,1,0:T(8,128)(2,1)} %coeff.1, bf16[4,128,128]{2,1,0:T(8,128)(2,1)} %amps.1, s32[4,256]{1,0:T(4,128)} %dom.1, s32[4,12]{1,0:T(4,128)} %partners.1, f32[4,12]{1,0:T(4,128)} %couplings.1), custom_call_target="tpu_custom_call" | custom-call | tf_op jit(solution)/shard_map/pack/pallas_call | solution.py:118
  2.0 3.1 %collective-permute-start.5 = (bf16[4,272,128]{2,1,0:T(8,128)(2,1)}, bf16[4,272,128]{2,1,0:T(8,128)(2,1)S(1)}, u32[]{:S(2)}, u32[]{:S(2)}) collective-permute-start(bf16[4,272,128]{2,1,0:T(8,128)(2,1)} %get-tuple-element.7.sent), channel_id=1, source_target_pairs={{3,0},{0,1},{1,2},{2,3},{7,4},{4,5},{5,6},{6,7},{11,8},{8,9},{9,10... | collective-permute-start | bytes 835592 | tf_op jit(solution)/shard_map/ppermute | solution.py:142
  5.1 2.0 %collective-permute-start.3 = (bf16[4,272,128]{2,1,0:T(8,128)(2,1)}, bf16[4,272,128]{2,1,0:T(8,128)(2,1)S(1)}, u32[]{:S(2)}, u32[]{:S(2)}) collective-permute-start(bf16[4,272,128]{2,1,0:T(8,128)(2,1)} %get-tuple-element.7.sent), channel_id=1, source_target_pairs={{1,0},{2,1},{3,2},{0,3},{5,4},{6,5},{7,6},{4,7},{9,8},{10,9},{11,1... | collective-permute-start | bytes 835592 | tf_op jit(solution)/shard_map/ppermute | solution.py:142
  7.1 1.0 %collective-permute-start.1 = (bf16[4,272,128]{2,1,0:T(8,128)(2,1)}, bf16[4,272,128]{2,1,0:T(8,128)(2,1)S(1)}, u32[]{:S(2)}, u32[]{:S(2)}) collective-permute-start(bf16[4,272,128]{2,1,0:T(8,128)(2,1)} %get-tuple-element.7.sent), channel_id=1, source_target_pairs={{2,0},{3,1},{0,2},{1,3},{6,4},{7,5},{4,6},{5,7},{10,8},{11,9},{8,1... | collective-permute-start | bytes 835592 | tf_op jit(solution)/shard_map/ppermute | solution.py:142
  8.1 1.3 %collective-permute-start = (bf16[4,400,128]{2,1,0:T(8,128)(2,1)}, bf16[4,400,128]{2,1,0:T(8,128)(2,1)S(1)}, u32[]{:S(2)}, u32[]{:S(2)}) collective-permute-start(bf16[4,400,128]{2,1,0:T(8,128)(2,1)} %get-tuple-element.8.near), channel_id=1, source_target_pairs={{2,6},{3,7},{4,0},{5,1},{6,10},{7,11},{8,4},{9,5},{10,14},{11,15},... | collective-permute-start | bytes 1228808 | tf_op jit(solution)/shard_map/ppermute | solution.py:138
  9.4 0.6 %pad_add_fusion.3.ids = s32[2]{0:T(128)} fusion(s32[1]{0:T(128)} %bitcast.5, s32[1]{0:T(128)} %bitcast), kind=kLoop, calls=%fused_computation.6 | loop fusion | flops 2 | bytes 16 | tf_op jit(solution)/shard_map/stack | solution.py:147
  10.0 0.6 %pad_add_fusion.2.ids = s32[2]{0:T(128)} fusion(s32[1]{0:T(128)} %bitcast.4, s32[1]{0:T(128)} %bitcast), kind=kLoop, calls=%fused_computation.5 | loop fusion | flops 2 | bytes 16 | tf_op jit(solution)/shard_map/stack | solution.py:147
  10.7 0.6 pad_add_fusion.1.ids
  11.3 8.6 %fusion.exchange = f32[16,128,128]{2,1,0:T(8,128)} fusion(bf16[1024,16,128]{2,1,0:T(8,128)(2,1)} %param.7), kind=kOutput, calls=%fused_computation | convolution fusion | flops 536870912 | bytes 5242880 | tf_op jit(solution)/shard_map/xpa,xpb->pab/dot_general | solution.py:144
  19.9 0.0 copy-start.1
  19.9 0.0 copy-start.5
  19.9 0.0 collective-permute-done.5.sent
  19.9 0.0 copy-start.4
  19.9 0.0 collective-permute-done.beside
  19.9 0.7 %copy-done.4 = bf16[4,272,128]{2,1,0:T(8,128)(2,1)} copy-done((bf16[4,272,128]{2,1,0:T(8,128)(2,1)}, bf16[4,272,128]{2,1,0:T(8,128)(2,1)S(1)}, u32[]{:S(2)}) %copy-start.4) | copy-done | bytes 278552
  20.6 0.0 copy-start
  20.6 0.8 %copy-done = bf16[4,400,128]{2,1,0:T(8,128)(2,1)} copy-done((bf16[4,400,128]{2,1,0:T(8,128)(2,1)}, bf16[4,400,128]{2,1,0:T(8,128)(2,1)S(1)}, u32[]{:S(2)}) %copy-start) | copy-done | bytes 409624
  21.4 5.7 %terms.7 = bf16[4,128,128]{2,1,0:T(8,128)(2,1)} custom-call(s32[2]{0:T(128)} %pad_add_fusion.3.ids, bf16[4,272,128]{2,1,0:T(8,128)(2,1)} %copy-done.4, bf16[4,400,128]{2,1,0:T(8,128)(2,1)} %get-tuple-element.8.near, bf16[4,400,128]{2,1,0:T(8,128)(2,1)} %copy-done, f32[16,128,128]{2,1,0:T(8,128)} %fusion.exchange), custom_call_target="tpu_custom_call" | custom-call | tf_op jit(solution)/shard_map/terms/pallas_call | solution.py:149
  27.0 1.9 %collective-permute-start.6 = (bf16[4,128,128]{2,1,0:T(8,128)(2,1)}, bf16[4,128,128]{2,1,0:T(8,128)(2,1)S(1)}, u32[]{:S(2)}, u32[]{:S(2)}) collective-permute-start(bf16[4,128,128]{2,1,0:T(8,128)(2,1)} %terms.7), channel_id=1, source_target_pairs={{0,3},{1,0},{2,1},{3,2},{4,7},{5,4},{6,5},{7,6},{8,11},{9,8},{10,9... | collective-permute-start | bytes 393224 | tf_op jit(solution)/shard_map/ppermute | solution.py:165
  28.9 0.0 collective-permute-done.3.sent
  28.9 0.0 copy-start.3
  28.9 0.7 %copy-done.3 = bf16[4,272,128]{2,1,0:T(8,128)(2,1)} copy-done((bf16[4,272,128]{2,1,0:T(8,128)(2,1)}, bf16[4,272,128]{2,1,0:T(8,128)(2,1)S(1)}, u32[]{:S(2)}) %copy-start.3) | copy-done | bytes 278552
  29.7 5.7 %terms.6 = bf16[4,128,128]{2,1,0:T(8,128)(2,1)} custom-call(s32[2]{0:T(128)} %pad_add_fusion.2.ids, bf16[4,272,128]{2,1,0:T(8,128)(2,1)} %copy-done.3, bf16[4,400,128]{2,1,0:T(8,128)(2,1)} %get-tuple-element.8.near, bf16[4,400,128]{2,1,0:T(8,128)(2,1)} %copy-done, f32[16,128,128]{2,1,0:T(8,128)} %fusion.exchange), custom_call_target="tpu_custom_call" | custom-call | tf_op jit(solution)/shard_map/terms/pallas_call | solution.py:149
  35.3 4.2 %collective-permute-start.4 = (bf16[4,128,128]{2,1,0:T(8,128)(2,1)}, bf16[4,128,128]{2,1,0:T(8,128)(2,1)S(1)}, u32[]{:S(2)}, u32[]{:S(2)}) collective-permute-start(bf16[4,128,128]{2,1,0:T(8,128)(2,1)} %terms.6), channel_id=1, source_target_pairs={{0,1},{1,2},{2,3},{3,0},{4,5},{5,6},{6,7},{7,4},{8,9},{9,10},{10,1... | collective-permute-start | bytes 393224 | tf_op jit(solution)/shard_map/ppermute | solution.py:165
  39.5 0.0 collective-permute-done.1.sent
  39.5 0.0 copy-start.2
  39.5 0.7 %copy-done.2 = bf16[4,272,128]{2,1,0:T(8,128)(2,1)} copy-done((bf16[4,272,128]{2,1,0:T(8,128)(2,1)}, bf16[4,272,128]{2,1,0:T(8,128)(2,1)S(1)}, u32[]{:S(2)}) %copy-start.2) | copy-done | bytes 278552
  40.2 5.7 %terms.5 = bf16[4,128,128]{2,1,0:T(8,128)(2,1)} custom-call(s32[2]{0:T(128)} %pad_add_fusion.1.ids, bf16[4,272,128]{2,1,0:T(8,128)(2,1)} %copy-done.2, bf16[4,400,128]{2,1,0:T(8,128)(2,1)} %get-tuple-element.8.near, bf16[4,400,128]{2,1,0:T(8,128)(2,1)} %copy-done, f32[16,128,128]{2,1,0:T(8,128)} %fusion.exchange), custom_call_target="tpu_custom_call" | custom-call | tf_op jit(solution)/shard_map/terms/pallas_call | solution.py:149
  45.9 3.8 %collective-permute-start.2 = (bf16[4,128,128]{2,1,0:T(8,128)(2,1)}, bf16[4,128,128]{2,1,0:T(8,128)(2,1)S(1)}, u32[]{:S(2)}, u32[]{:S(2)}) collective-permute-start(bf16[4,128,128]{2,1,0:T(8,128)(2,1)} %terms.5), channel_id=1, source_target_pairs={{0,2},{1,3},{2,0},{3,1},{4,6},{5,7},{6,4},{7,5},{8,10},{9,11},{10,... | collective-permute-start | bytes 393224 | tf_op jit(solution)/shard_map/ppermute | solution.py:165
  49.7 0.6 %pad_add_fusion.ids = s32[2]{0:T(128)} fusion(s32[1]{0:T(128)} %bitcast.1, s32[1]{0:T(128)} %bitcast), kind=kLoop, calls=%fused_computation.3 | loop fusion | flops 2 | bytes 16 | tf_op jit(solution)/shard_map/stack | solution.py:147
  50.3 5.7 %terms.4 = f32[4,128,128]{2,1,0:T(8,128)} custom-call(s32[2]{0:T(128)} %pad_add_fusion.ids, bf16[4,272,128]{2,1,0:T(8,128)(2,1)} %get-tuple-element.7.sent, bf16[4,400,128]{2,1,0:T(8,128)(2,1)} %get-tuple-element.8.near, bf16[4,400,128]{2,1,0:T(8,128)(2,1)} %copy-done, f32[16,128,128]{2,1,0:T(8,128)} %fusion.exchange), custom_call_target="tpu_custom_call" | custom-call | tf_op jit(solution)/shard_map/terms/pallas_call | solution.py:149
  56.1 0.0 collective-permute-done.6
  56.1 0.0 collective-permute-done.4
  56.1 0.0 collective-permute-done.2
  56.1 0.0 copy-done.1
  56.1 0.0 copy-done.5
  56.1 1.8 %convert_add_fusion = f32[4,128,128]{2,1,0:T(8,128)} fusion(bf16[4,128,128]{2,1,0:T(8,128)(2,1)S(1)} %collective-permute-done.6, bf16[4,128,128]{2,1,0:T(8,128)(2,1)S(1)} %collective-permute-done.4, bf16[4,128,128]{2,1,0:T(8,128)(2,1)S(1)} %collective-permute-done.2, f32[4,128,128]{2,1,0:T(8,128)} %terms.4, bf16[4,128,128]{2,1,0:T(8,128)(2,1)S(1)} %copy-done.1, ...), kind=kLoop, calls=%fused_computation.2 | loop fusion | flops 655360 | bytes 1050624 | tf_op jit(solution)/shard_map/add | solution.py:171
Async XLA Ops:
  2.0 17.9 %collective-permute-start.5 = (bf16[4,272,128]{2,1,0:T(8,128)(2,1)}, bf16[4,272,128]{2,1,0:T(8,128)(2,1)S(1)}, u32[]{:S(2)}, u32[]{:S(2)}) collective-permute-start(bf16[4,272,128]{2,1,0:T(8,128)(2,1)} %get-tuple-element.7.sent), channel_id=1, source_target_pairs={{3,0},{0,1},{1,2},{2,3},{7,4},{4,5},{5,6},{6,7},{11,8},{8,9},{9,10... | collective-permute-start | bytes 835592 | tf_op jit(solution)/shard_map/ppermute | solution.py:142
  5.1 23.9 %collective-permute-start.3 = (bf16[4,272,128]{2,1,0:T(8,128)(2,1)}, bf16[4,272,128]{2,1,0:T(8,128)(2,1)S(1)}, u32[]{:S(2)}, u32[]{:S(2)}) collective-permute-start(bf16[4,272,128]{2,1,0:T(8,128)(2,1)} %get-tuple-element.7.sent), channel_id=1, source_target_pairs={{1,0},{2,1},{3,2},{0,3},{5,4},{6,5},{7,6},{4,7},{9,8},{10,9},{11,1... | collective-permute-start | bytes 835592 | tf_op jit(solution)/shard_map/ppermute | solution.py:142
  7.1 32.4 %collective-permute-start.1 = (bf16[4,272,128]{2,1,0:T(8,128)(2,1)}, bf16[4,272,128]{2,1,0:T(8,128)(2,1)S(1)}, u32[]{:S(2)}, u32[]{:S(2)}) collective-permute-start(bf16[4,272,128]{2,1,0:T(8,128)(2,1)} %get-tuple-element.7.sent), channel_id=1, source_target_pairs={{2,0},{3,1},{0,2},{1,3},{6,4},{7,5},{4,6},{5,7},{10,8},{11,9},{8,1... | collective-permute-start | bytes 835592 | tf_op jit(solution)/shard_map/ppermute | solution.py:142
  8.1 11.8 %collective-permute-start = (bf16[4,400,128]{2,1,0:T(8,128)(2,1)}, bf16[4,400,128]{2,1,0:T(8,128)(2,1)S(1)}, u32[]{:S(2)}, u32[]{:S(2)}) collective-permute-start(bf16[4,400,128]{2,1,0:T(8,128)(2,1)} %get-tuple-element.8.near), channel_id=1, source_target_pairs={{2,6},{3,7},{4,0},{5,1},{6,10},{7,11},{8,4},{9,5},{10,14},{11,15},... | collective-permute-start | bytes 1228808 | tf_op jit(solution)/shard_map/ppermute | solution.py:138
  19.9 36.2 %copy-start.1 = (bf16[4,128,128]{2,1,0:T(8,128)(2,1)S(1)}, bf16[4,128,128]{2,1,0:T(8,128)(2,1)}, u32[]{:S(2)}) copy-start(bf16[4,128,128]{2,1,0:T(8,128)(2,1)} %amps.1) | copy-start | bytes 393220
  19.9 36.2 %copy-start.5 = (f32[4,128]{1,0:T(4,128)S(1)}, f32[4,128]{1,0:T(4,128)}, u32[]{:S(2)}) copy-start(f32[4,128]{1,0:T(4,128)} %param.13) | copy-start | bytes 6148
  19.9 0.7 %copy-start.4 = (bf16[4,272,128]{2,1,0:T(8,128)(2,1)}, bf16[4,272,128]{2,1,0:T(8,128)(2,1)S(1)}, u32[]{:S(2)}) copy-start(bf16[4,272,128]{2,1,0:T(8,128)(2,1)S(1)} %collective-permute-done.5.sent) | copy-start | bytes 835588
  20.6 0.8 %copy-start = (bf16[4,400,128]{2,1,0:T(8,128)(2,1)}, bf16[4,400,128]{2,1,0:T(8,128)(2,1)S(1)}, u32[]{:S(2)}) copy-start(bf16[4,400,128]{2,1,0:T(8,128)(2,1)S(1)} %collective-permute-done.beside) | copy-start | bytes 1228804
  27.0 29.0 %collective-permute-start.6 = (bf16[4,128,128]{2,1,0:T(8,128)(2,1)}, bf16[4,128,128]{2,1,0:T(8,128)(2,1)S(1)}, u32[]{:S(2)}, u32[]{:S(2)}) collective-permute-start(bf16[4,128,128]{2,1,0:T(8,128)(2,1)} %terms.7), channel_id=1, source_target_pairs={{0,3},{1,0},{2,1},{3,2},{4,7},{5,4},{6,5},{7,6},{8,11},{9,8},{10,9... | collective-permute-start | bytes 393224 | tf_op jit(solution)/shard_map/ppermute | solution.py:165
  28.9 0.7 %copy-start.3 = (bf16[4,272,128]{2,1,0:T(8,128)(2,1)}, bf16[4,272,128]{2,1,0:T(8,128)(2,1)S(1)}, u32[]{:S(2)}) copy-start(bf16[4,272,128]{2,1,0:T(8,128)(2,1)S(1)} %collective-permute-done.3.sent) | copy-start | bytes 835588
  35.3 20.7 %collective-permute-start.4 = (bf16[4,128,128]{2,1,0:T(8,128)(2,1)}, bf16[4,128,128]{2,1,0:T(8,128)(2,1)S(1)}, u32[]{:S(2)}, u32[]{:S(2)}) collective-permute-start(bf16[4,128,128]{2,1,0:T(8,128)(2,1)} %terms.6), channel_id=1, source_target_pairs={{0,1},{1,2},{2,3},{3,0},{4,5},{5,6},{6,7},{7,4},{8,9},{9,10},{10,1... | collective-permute-start | bytes 393224 | tf_op jit(solution)/shard_map/ppermute | solution.py:165
  39.5 0.7 %copy-start.2 = (bf16[4,272,128]{2,1,0:T(8,128)(2,1)}, bf16[4,272,128]{2,1,0:T(8,128)(2,1)S(1)}, u32[]{:S(2)}) copy-start(bf16[4,272,128]{2,1,0:T(8,128)(2,1)S(1)} %collective-permute-done.1.sent) | copy-start | bytes 835588
  45.9 10.1 %collective-permute-start.2 = (bf16[4,128,128]{2,1,0:T(8,128)(2,1)}, bf16[4,128,128]{2,1,0:T(8,128)(2,1)S(1)}, u32[]{:S(2)}, u32[]{:S(2)}) collective-permute-start(bf16[4,128,128]{2,1,0:T(8,128)(2,1)} %terms.5), channel_id=1, source_target_pairs={{0,2},{1,3},{2,0},{3,1},{4,6},{5,7},{6,4},{7,5},{8,10},{9,11},{10,... | collective-permute-start | bytes 393224 | tf_op jit(solution)/shard_map/ppermute | solution.py:165

commit v2 on v1

--- a/solution.py
+++ b/solution.py
@@ -9,7 +9,14 @@
 
 BF16 = jnp.bfloat16
 F32 = jnp.float32
+GRANT = 16 << 20
 WHOLE = pl.BlockSpec(memory_space=pltpu.VMEM)
+SMEM = pl.BlockSpec(memory_space=pltpu.SMEM)
+FAR = pl.BlockSpec(memory_space=pltpu.HBM)
+
+
+def kept(array):
+    return pltpu.with_memory_space_constraint(array, pltpu.VMEM)
 
 
 def meta_rows(dom_width, lanes, weight_count):
@@ -17,9 +24,19 @@
     return -(-rows // 16) * 16
 
 
-def pack_body(ids, coeff, amps, dom, partners, couplings, sent, hosted, *, aux_count):
+def pack_body(ids, coeff, amps, dom, partners, couplings, sent, hosted, funcs_at, listed_at, strength_at, sems, *, aux_count):
     own, width, lanes = coeff.shape
     slots = 2 * own
+    extra = meta_rows(width, lanes, aux_count * slots)
+    moves = [
+        (listed_at, partners), (strength_at, couplings), (funcs_at, dom),
+        (sent.at[:, :width], coeff), (hosted.at[:, :width], coeff), (hosted.at[:, width + extra :], amps),
+    ]
+    copies = [pltpu.make_async_copy(src, dst, sems.at[k]) for k, (dst, src) in enumerate(moves)]
+    for copy in copies:
+        copy.start()
+    for copy in copies[:3]:
+        copy.wait()
     group = own * aux_count
     weight_rows = -(-aux_count * slots // lanes)
     at = lax.broadcasted_iota(jnp.int32, (1, weight_rows * lanes), 1)
@@ -28,16 +45,15 @@
     beside = jnp.where(host < aux_count // 2, group, -group)
     number = jnp.where(slot < own, first + slot, first + slot - own + beside)
     number = jnp.where(host < aux_count, number, -1)
-    listed, strength = partners[...], couplings[...]
+    listed, strength = listed_at[...], strength_at[...]
     weight = jnp.zeros((own, weight_rows * lanes), F32)
     for c in range(listed.shape[1]):
         weight += jnp.where(listed[:, c : c + 1] == number, strength[:, c : c + 1], 0.0)
     coarse = weight.astype(BF16).astype(F32)
     fine = weight - coarse
-    funcs = dom[...]
+    funcs = funcs_at[...]
     high = (funcs >> 8).astype(F32)
     low = (funcs & 255).astype(F32)
-    extra = meta_rows(width, lanes, aux_count * slots)
     for p in range(own):
         rows = []
         for part in (high, low, coarse, fine):
@@ -45,12 +61,10 @@
                 rows.append(part[p : p + 1, k * lanes : (k + 1) * lanes])
         rows.append(jnp.zeros((extra - len(rows), lanes), F32))
         meta = jnp.concatenate(rows, axis=0).astype(BF16)
-        orbitals = coeff[p]
-        sent[p, :width] = orbitals
         sent[p, width:] = meta
-        hosted[p, :width] = orbitals
         hosted[p, width : width + extra] = meta
-        hosted[p, width + extra :] = amps[p]
+    for copy in copies[3:]:
+        copy.wait()
 
 
 def functions_of(meta, width, lanes):
@@ -58,8 +72,9 @@
     return [meta[k : k + 1] * 256.0 + meta[parts + k : parts + k + 1] for k in range(parts)]
 
 
-def terms_body(ids, sent, near, beside, exchange, out, *, width):
+def terms_body(ids, sent, near, beside, exchange, out, *, width, shift, aux_count):
     own, _, lanes = sent.shape
+    target = lax.rem(ids[0] + shift, aux_count) * own
     extra = sent.shape[1] - width
     slots = 2 * own
     parts = width // lanes
@@ -102,7 +117,7 @@
             (((1,), (1,)), ((), ())),
             preferred_element_type=F32,
         )
-        out[p] = (exchange[p] - coupled).astype(out.dtype)
+        out[p] = (exchange[target + p] - coupled).astype(out.dtype)
 
 
 def shards(factors, coefficients, amplitudes, domains, partners, couplings, energies):
@@ -113,20 +128,29 @@
     extra = meta_rows(width, lanes, aux_count * 2 * own)
     group_at = lax.axis_index("pairs")
     aux_at = lax.axis_index("aux")
-    smem = pl.BlockSpec(memory_space=pltpu.SMEM)
 
     sent, hosted = pl.pallas_call(
         functools.partial(pack_body, aux_count=aux_count),
         out_shape=(
-            jax.ShapeDtypeStruct((own, width + extra, lanes), BF16),
-            jax.ShapeDtypeStruct((own, width + extra + lanes, lanes), BF16),
+            pltpu.VMEM((own, width + extra, lanes), BF16),
+            pltpu.VMEM((own, width + extra + lanes, lanes), BF16),
         ),
-        in_specs=[smem, WHOLE, WHOLE, WHOLE, WHOLE, WHOLE],
+        in_specs=[SMEM, FAR, FAR, FAR, FAR, FAR],
         out_specs=(WHOLE, WHOLE),
+        scratch_shapes=[
+            pltpu.VMEM(domains.shape, domains.dtype),
+            pltpu.VMEM(partners.shape, partners.dtype),
+            pltpu.VMEM(couplings.shape, couplings.dtype),
+            pltpu.SemaphoreType.DMA((6,)),
+        ],
+        compiler_params=pltpu.CompilerParams(vmem_limit_bytes=GRANT),
         name="pack",
     )(
         (group_at * own * aux_count).reshape(1).astype(jnp.int32),
-        coefficients, amplitudes, domains, partners, couplings,
+        *(
+            pltpu.with_memory_space_constraint(a, pltpu.HBM)
+            for a in (coefficients, amplitudes, domains, partners, couplings)
+        ),
     )
 
     routes = []
@@ -143,23 +167,18 @@
 
     exchange = jnp.einsum("xpa,xpb->pab", factors, factors, preferred_element_type=F32)
 
+    exchange, beside = kept(exchange), kept(beside)
+    place = aux_at.reshape(1).astype(jnp.int32)
+
     def terms(s, dtype):
-        ids = jnp.stack([aux_at, (aux_at + s) % aux_count]).astype(jnp.int32)
-        whole = lambda a: pl.BlockSpec(a.shape, lambda i, ids: (0,) * a.ndim)
         return pl.pallas_call(
-            functools.partial(terms_body, width=width),
-            grid_spec=pltpu.PrefetchScalarGridSpec(
-                num_scalar_prefetch=1,
-                grid=(1,),
-                in_specs=[
-                    whole(arrived[s]), whole(hosted), whole(beside),
-                    pl.BlockSpec((own, lanes, lanes), lambda i, ids: (ids[1], 0, 0)),
-                ],
-                out_specs=pl.BlockSpec((own, lanes, lanes), lambda i, ids: (0, 0, 0)),
-            ),
-            out_shape=jax.ShapeDtypeStruct((own, lanes, lanes), dtype),
+            functools.partial(terms_body, width=width, shift=s, aux_count=aux_count),
+            in_specs=[SMEM, WHOLE, WHOLE, WHOLE, WHOLE],
+            out_specs=WHOLE,
+            out_shape=pltpu.VMEM((own, lanes, lanes), dtype),
+            compiler_params=pltpu.CompilerParams(vmem_limit_bytes=GRANT),
             name="terms",
-        )(ids, arrived[s], hosted, beside, exchange)
+        )(place, kept(arrived[s]), kept(hosted), beside, exchange)
 
     returned = [
         lax.ppermute(terms(s, BF16), "aux", [(i, (i + s) % aux_count) for i in range(aux_count)])

time: 58.3 us -> 45.8 us (0.79)
  Pallas kernels: 24.8 us -> 13.6 us
  other arithmetic: 4.25 us -> 0.88 us
  starting transfers between devices: 17.3 us -> 20.6 us
  local copies, waits for them, and re-layouts: 2.9 us -> 0.01 us
  waiting for transfers between devices: 0.02 us -> 2.78 us
  matrix products: 8.62 us -> 7.64 us
    pallas_call x4, Pallas kernels: 22.8 us -> 12.4 us  [terms(): pl.pallas_call(functools.partial(terms_body, width=width, shift=s, aux_co...]
    ppermute x3, starting transfers between devices: 9.89 us -> 13.2 us  [shards(): lax.ppermute(terms(s, BF16), 'aux', [(i, (i + s) % aux_count) for i in ra...]
    unnamed x12 -> x4, local copies, waits for them, and re-layouts: 2.9 us -> 0.01 us
    another operation x4 -> x0, other arithmetic: 2.42 us -> none  [terms(): ids = jnp.stack([aux_at, (aux_at + s) % aux_count]).astype(jnp.int32)]
    ppermute x3, waiting for transfers between devices: 0.01 us -> 1.71 us  [shards(): lax.ppermute(terms(s, BF16), 'aux', [(i, (i + s) % aux_count) for i in ra...]
    ppermute x3, waiting for transfers between devices: 0.01 us -> 1.06 us  [shards(): lax.ppermute(sent, 'aux', [((i + s) % aux_count, i) for i in range(aux_co...]
    dot_general x1, matrix products: 8.62 us -> 7.64 us  [shards(): jnp.einsum('xpa,xpb->pab', factors, factors, preferred_element_type=F32)]
    add x1, other arithmetic: 1.83 us -> 0.88 us  [shards(): total += part.astype(F32)]
  transfers between devices with their start and end apart: 7 -> 7, of which waited for: 0 -> 2; matrix products, arithmetic and copies ran while one was open for 19% -> 17% of each run, Pallas kernels for 39% -> 27%
where the time goes in v2:
time: 45.8 us; the launch traced here: 45.6 us
  starting transfers between devices  20.6 us (45%)
  Pallas kernels  13.6 us (30%)
  matrix products  7.64 us (17%)
  waiting for transfers between devices  2.78 us (6%)
  other arithmetic  0.88 us (2%)
    ppermute x3, starting transfers between devices, shards(): lax.ppermute(terms(s, BF16), 'aux', [(i, (i + s) % aux_count) for i in ra...  13.2 us
    pallas_call x4, Pallas kernels, terms(): pl.pallas_call(functools.partial(terms_body, width=width, shift=s, aux_co...  12.4 us
    dot_general x1, matrix products, shards(): jnp.einsum('xpa,xpb->pab', factors, factors, preferred_element_type=F32)  7.64 us
    ppermute x3, starting transfers between devices, shards(): lax.ppermute(sent, 'aux', [((i + s) % aux_count, i) for i in range(aux_co...  6.14 us
    ppermute x3, waiting for transfers between devices, shards(): lax.ppermute(terms(s, BF16), 'aux', [(i, (i + s) % aux_count) for i in ra...  1.71 us
    ppermute x1, starting transfers between devices, shards(): beside = lax.ppermute(hosted, ('pairs', 'aux'), routes)  1.28 us
    pallas_call x1, Pallas kernels, shards(): pl.pallas_call(functools.partial(pack_body, aux_count=aux_count), out_sha...  1.16 us
    ppermute x3, waiting for transfers between devices, shards(): lax.ppermute(sent, 'aux', [((i + s) % aux_count, i) for i in range(aux_co...  1.06 us
  transfers between devices with their start and end apart: 7, of which 2 were waited for; matrix products, arithmetic and copies ran while one was open for 17% of the time, Pallas kernels for 27%

profile of v2, /device:TPU:0, one launch (start us, length us, event | category | flops | bytes accessed | tf_op | source)
XLA Modules:
  0.0 45.6 jit_solution(16770868262679929017)
XLA Ops:
  0.0 1.2 %pack.1 = (bf16[4,272,128]{2,1,0:T(8,128)(2,1)S(1)}, bf16[4,400,128]{2,1,0:T(8,128)(2,1)S(1)}) custom-call(s32[1]{0:T(128)} %bitcast.1.ids, bf16[4,256,128]{2,1,0:T(8,128)(2,1)} %coeff.1, bf16[4,128,128]{2,1,0:T(8,128)(2,1)} %amps.1, s32[4,256]{1,0:T(4,128)} %dom.1, s32[4,12]{1,0:T(4,128)} %partners.1, f32[4,12]{1,0:T(4,128)} %couplings.1), custom_call_target="tpu_custom_call" | custom-call | tf_op jit(solution)/shard_map/pack/pallas_call | solution.py:132
  1.2 3.1 %collective-permute-start.5 = (bf16[4,272,128]{2,1,0:T(8,128)(2,1)S(1)}, bf16[4,272,128]{2,1,0:T(8,128)(2,1)S(1)}, u32[]{:S(2)}, u32[]{:S(2)}) collective-permute-start(bf16[4,272,128]{2,1,0:T(8,128)(2,1)S(1)} %get-tuple-element.7.sent), channel_id=1, source_target_pairs={{3,0},{0,1},{1,2},{2,3},{7,4},{4,5},{5,6},{6,7},{11,8},{8,9},{9,10... | collective-permute-start | bytes 835592 | tf_op jit(solution)/shard_map/ppermute | solution.py:166
  4.3 2.1 %collective-permute-start.3 = (bf16[4,272,128]{2,1,0:T(8,128)(2,1)S(1)}, bf16[4,272,128]{2,1,0:T(8,128)(2,1)S(1)}, u32[]{:S(2)}, u32[]{:S(2)}) collective-permute-start(bf16[4,272,128]{2,1,0:T(8,128)(2,1)S(1)} %get-tuple-element.7.sent), channel_id=1, source_target_pairs={{1,0},{2,1},{3,2},{0,3},{5,4},{6,5},{7,6},{4,7},{9,8},{10,9},{11,1... | collective-permute-start | bytes 835592 | tf_op jit(solution)/shard_map/ppermute | solution.py:166
  6.4 0.9 %collective-permute-start.1 = (bf16[4,272,128]{2,1,0:T(8,128)(2,1)S(1)}, bf16[4,272,128]{2,1,0:T(8,128)(2,1)S(1)}, u32[]{:S(2)}, u32[]{:S(2)}) collective-permute-start(bf16[4,272,128]{2,1,0:T(8,128)(2,1)S(1)} %get-tuple-element.7.sent), channel_id=1, source_target_pairs={{2,0},{3,1},{0,2},{1,3},{6,4},{7,5},{4,6},{5,7},{10,8},{11,9},{8,1... | collective-permute-start | bytes 835592 | tf_op jit(solution)/shard_map/ppermute | solution.py:166
  7.3 1.3 %collective-permute-start = (bf16[4,400,128]{2,1,0:T(8,128)(2,1)S(1)}, bf16[4,400,128]{2,1,0:T(8,128)(2,1)S(1)}, u32[]{:S(2)}, u32[]{:S(2)}) collective-permute-start(bf16[4,400,128]{2,1,0:T(8,128)(2,1)S(1)} %get-tuple-element.8.near), channel_id=1, source_target_pairs={{2,6},{3,7},{4,0},{5,1},{6,10},{7,11},{8,4},{9,5},{10,14},{11,15},... | collective-permute-start | bytes 1228808 | tf_op jit(solution)/shard_map/ppermute | solution.py:162
  8.6 7.6 %fusion.exchange = f32[16,128,128]{2,1,0:T(8,128)S(1)} fusion(bf16[1024,16,128]{2,1,0:T(8,128)(2,1)} %param.7), kind=kOutput, calls=%fused_computation | convolution fusion | flops 536870912 | bytes 5242880 | tf_op jit(solution)/shard_map/xpa,xpb->pab/dot_general | solution.py:168
  16.2 0.0 collective-permute-done.5.sent
  16.3 0.0 collective-permute-done.beside
  16.3 0.0 copy-start
  16.3 0.0 copy-start.1
  16.3 3.1 %terms.7 = bf16[4,128,128]{2,1,0:T(8,128)(2,1)S(1)} custom-call(s32[1]{0:T(128)} %bitcast.ids, bf16[4,272,128]{2,1,0:T(8,128)(2,1)S(1)} %collective-permute-done.5.sent, bf16[4,400,128]{2,1,0:T(8,128)(2,1)S(1)} %get-tuple-element.8.near, bf16[4,400,128]{2,1,0:T(8,128)(2,1)S(1)} %collective-permute-done.beside, f32[16,128,128]{2,1,0:T(8,128)S(1)} %fusion.exchange), custom_call_target="tpu_custom_call" | custom-call | tf_op jit(solution)/shard_map/terms/pallas_call | solution.py:174
  19.4 4.5 %collective-permute-start.6 = (bf16[4,128,128]{2,1,0:T(8,128)(2,1)S(1)}, bf16[4,128,128]{2,1,0:T(8,128)(2,1)S(1)}, u32[]{:S(2)}, u32[]{:S(2)}) collective-permute-start(bf16[4,128,128]{2,1,0:T(8,128)(2,1)S(1)} %terms.7), channel_id=1, source_target_pairs={{0,3},{1,0},{2,1},{3,2},{4,7},{5,4},{6,5},{7,6},{8,11},{9,8},{10,9... | collective-permute-start | bytes 393224 | tf_op jit(solution)/shard_map/ppermute | solution.py:184
  23.9 0.0 collective-permute-done.3.sent
  23.9 3.1 %terms.6 = bf16[4,128,128]{2,1,0:T(8,128)(2,1)S(1)} custom-call(s32[1]{0:T(128)} %bitcast.ids, bf16[4,272,128]{2,1,0:T(8,128)(2,1)S(1)} %collective-permute-done.3.sent, bf16[4,400,128]{2,1,0:T(8,128)(2,1)S(1)} %get-tuple-element.8.near, bf16[4,400,128]{2,1,0:T(8,128)(2,1)S(1)} %collective-permute-done.beside, f32[16,128,128]{2,1,0:T(8,128)S(1)} %fusion.exchange), custom_call_target="tpu_custom_call" | custom-call | tf_op jit(solution)/shard_map/terms/pallas_call | solution.py:174
  27.0 4.3 %collective-permute-start.4 = (bf16[4,128,128]{2,1,0:T(8,128)(2,1)S(1)}, bf16[4,128,128]{2,1,0:T(8,128)(2,1)S(1)}, u32[]{:S(2)}, u32[]{:S(2)}) collective-permute-start(bf16[4,128,128]{2,1,0:T(8,128)(2,1)S(1)} %terms.6), channel_id=1, source_target_pairs={{0,1},{1,2},{2,3},{3,0},{4,5},{5,6},{6,7},{7,4},{8,9},{9,10},{10,1... | collective-permute-start | bytes 393224 | tf_op jit(solution)/shard_map/ppermute | solution.py:184
  31.3 1.1 %collective-permute-done.1.sent = bf16[4,272,128]{2,1,0:T(8,128)(2,1)S(1)} collective-permute-done((bf16[4,272,128]{2,1,0:T(8,128)(2,1)S(1)}, bf16[4,272,128]{2,1,0:T(8,128)(2,1)S(1)}, u32[]{:S(2)}, u32[]{:S(2)}) %collective-permute-start.1) | collective-permute-done | bytes 278560 | tf_op jit(solution)/shard_map/ppermute | solution.py:166
  32.4 3.1 %terms.5 = bf16[4,128,128]{2,1,0:T(8,128)(2,1)S(1)} custom-call(s32[1]{0:T(128)} %bitcast.ids, bf16[4,272,128]{2,1,0:T(8,128)(2,1)S(1)} %collective-permute-done.1.sent, bf16[4,400,128]{2,1,0:T(8,128)(2,1)S(1)} %get-tuple-element.8.near, bf16[4,400,128]{2,1,0:T(8,128)(2,1)S(1)} %collective-permute-done.beside, f32[16,128,128]{2,1,0:T(8,128)S(1)} %fusion.exchange), custom_call_target="tpu_custom_call" | custom-call | tf_op jit(solution)/shard_map/terms/pallas_call | solution.py:174
  35.5 4.4 %collective-permute-start.2 = (bf16[4,128,128]{2,1,0:T(8,128)(2,1)S(1)}, bf16[4,128,128]{2,1,0:T(8,128)(2,1)S(1)}, u32[]{:S(2)}, u32[]{:S(2)}) collective-permute-start(bf16[4,128,128]{2,1,0:T(8,128)(2,1)S(1)} %terms.5), channel_id=1, source_target_pairs={{0,2},{1,3},{2,0},{3,1},{4,6},{5,7},{6,4},{7,5},{8,10},{9,11},{10,... | collective-permute-start | bytes 393224 | tf_op jit(solution)/shard_map/ppermute | solution.py:184
  39.9 3.1 %terms.4 = f32[4,128,128]{2,1,0:T(8,128)S(1)} custom-call(s32[1]{0:T(128)} %bitcast.ids, bf16[4,272,128]{2,1,0:T(8,128)(2,1)S(1)} %get-tuple-element.7.sent, bf16[4,400,128]{2,1,0:T(8,128)(2,1)S(1)} %get-tuple-element.8.near, bf16[4,400,128]{2,1,0:T(8,128)(2,1)S(1)} %collective-permute-done.beside, f32[16,128,128]{2,1,0:T(8,128)S(1)} %fusion.exchange), custom_call_target="tpu_custom_call" | custom-call | tf_op jit(solution)/shard_map/terms/pallas_call | solution.py:174
  43.0 0.0 collective-permute-done.6
  43.0 0.0 collective-permute-done.4
  43.0 1.7 %collective-permute-done.2 = bf16[4,128,128]{2,1,0:T(8,128)(2,1)S(1)} collective-permute-done((bf16[4,128,128]{2,1,0:T(8,128)(2,1)S(1)}, bf16[4,128,128]{2,1,0:T(8,128)(2,1)S(1)}, u32[]{:S(2)}, u32[]{:S(2)}) %collective-permute-start.2) | collective-permute-done | bytes 131104 | tf_op jit(solution)/shard_map/ppermute | solution.py:184
  44.7 0.0 copy-done
  44.7 0.0 copy-done.1
  44.7 0.9 %convert_add_fusion = f32[4,128,128]{2,1,0:T(8,128)} fusion(bf16[4,128,128]{2,1,0:T(8,128)(2,1)S(1)} %collective-permute-done.6, bf16[4,128,128]{2,1,0:T(8,128)(2,1)S(1)} %collective-permute-done.4, bf16[4,128,128]{2,1,0:T(8,128)(2,1)S(1)} %collective-permute-done.2, f32[4,128,128]{2,1,0:T(8,128)S(1)} %terms.4, bf16[4,128,128]{2,1,0:T(8,128)(2,1)S(1)} %copy-done, ...), kind=kLoop, calls=%fused_computation.2 | loop fusion | flops 655360 | bytes 1050624 | tf_op jit(solution)/shard_map/add | solution.py:190
Async XLA Ops:
  1.2 15.1 %collective-permute-start.5 = (bf16[4,272,128]{2,1,0:T(8,128)(2,1)S(1)}, bf16[4,272,128]{2,1,0:T(8,128)(2,1)S(1)}, u32[]{:S(2)}, u32[]{:S(2)}) collective-permute-start(bf16[4,272,128]{2,1,0:T(8,128)(2,1)S(1)} %get-tuple-element.7.sent), channel_id=1, source_target_pairs={{3,0},{0,1},{1,2},{2,3},{7,4},{4,5},{5,6},{6,7},{11,8},{8,9},{9,10... | collective-permute-start | bytes 835592 | tf_op jit(solution)/shard_map/ppermute | solution.py:166
  4.3 19.7 %collective-permute-start.3 = (bf16[4,272,128]{2,1,0:T(8,128)(2,1)S(1)}, bf16[4,272,128]{2,1,0:T(8,128)(2,1)S(1)}, u32[]{:S(2)}, u32[]{:S(2)}) collective-permute-start(bf16[4,272,128]{2,1,0:T(8,128)(2,1)S(1)} %get-tuple-element.7.sent), channel_id=1, source_target_pairs={{1,0},{2,1},{3,2},{0,3},{5,4},{6,5},{7,6},{4,7},{9,8},{10,9},{11,1... | collective-permute-start | bytes 835592 | tf_op jit(solution)/shard_map/ppermute | solution.py:166
  6.4 26.0 %collective-permute-start.1 = (bf16[4,272,128]{2,1,0:T(8,128)(2,1)S(1)}, bf16[4,272,128]{2,1,0:T(8,128)(2,1)S(1)}, u32[]{:S(2)}, u32[]{:S(2)}) collective-permute-start(bf16[4,272,128]{2,1,0:T(8,128)(2,1)S(1)} %get-tuple-element.7.sent), channel_id=1, source_target_pairs={{2,0},{3,1},{0,2},{1,3},{6,4},{7,5},{4,6},{5,7},{10,8},{11,9},{8,1... | collective-permute-start | bytes 835592 | tf_op jit(solution)/shard_map/ppermute | solution.py:166
  7.3 8.9 %collective-permute-start = (bf16[4,400,128]{2,1,0:T(8,128)(2,1)S(1)}, bf16[4,400,128]{2,1,0:T(8,128)(2,1)S(1)}, u32[]{:S(2)}, u32[]{:S(2)}) collective-permute-start(bf16[4,400,128]{2,1,0:T(8,128)(2,1)S(1)} %get-tuple-element.8.near), channel_id=1, source_target_pairs={{2,6},{3,7},{4,0},{5,1},{6,10},{7,11},{8,4},{9,5},{10,14},{11,15},... | collective-permute-start | bytes 1228808 | tf_op jit(solution)/shard_map/ppermute | solution.py:162
  16.3 28.4 %copy-start = (bf16[4,128,128]{2,1,0:T(8,128)(2,1)S(1)}, bf16[4,128,128]{2,1,0:T(8,128)(2,1)}, u32[]{:S(2)}) copy-start(bf16[4,128,128]{2,1,0:T(8,128)(2,1)} %amps.1) | copy-start | bytes 393220
  16.3 28.4 %copy-start.1 = (f32[4,128]{1,0:T(4,128)S(1)}, f32[4,128]{1,0:T(4,128)}, u32[]{:S(2)}) copy-start(f32[4,128]{1,0:T(4,128)} %param.13) | copy-start | bytes 6148
  19.4 23.6 %collective-permute-start.6 = (bf16[4,128,128]{2,1,0:T(8,128)(2,1)S(1)}, bf16[4,128,128]{2,1,0:T(8,128)(2,1)S(1)}, u32[]{:S(2)}, u32[]{:S(2)}) collective-permute-start(bf16[4,128,128]{2,1,0:T(8,128)(2,1)S(1)} %terms.7), channel_id=1, source_target_pairs={{0,3},{1,0},{2,1},{3,2},{4,7},{5,4},{6,5},{7,6},{8,11},{9,8},{10,9... | collective-permute-start | bytes 393224 | tf_op jit(solution)/shard_map/ppermute | solution.py:184
  27.0 15.9 %collective-permute-start.4 = (bf16[4,128,128]{2,1,0:T(8,128)(2,1)S(1)}, bf16[4,128,128]{2,1,0:T(8,128)(2,1)S(1)}, u32[]{:S(2)}, u32[]{:S(2)}) collective-permute-start(bf16[4,128,128]{2,1,0:T(8,128)(2,1)S(1)} %terms.6), channel_id=1, source_target_pairs={{0,1},{1,2},{2,3},{3,0},{4,5},{5,6},{6,7},{7,4},{8,9},{9,10},{10,1... | collective-permute-start | bytes 393224 | tf_op jit(solution)/shard_map/ppermute | solution.py:184
  35.5 9.2 %collective-permute-start.2 = (bf16[4,128,128]{2,1,0:T(8,128)(2,1)S(1)}, bf16[4,128,128]{2,1,0:T(8,128)(2,1)S(1)}, u32[]{:S(2)}, u32[]{:S(2)}) collective-permute-start(bf16[4,128,128]{2,1,0:T(8,128)(2,1)S(1)} %terms.5), channel_id=1, source_target_pairs={{0,2},{1,3},{2,0},{3,1},{4,6},{5,7},{6,4},{7,5},{8,10},{9,11},{10,... | collective-permute-start | bytes 393224 | tf_op jit(solution)/shard_map/ppermute | solution.py:184
